TPU v7x, 128 devices: a whole 4x4x4 slice. The times are simulated.
128 devices in a mesh: tm: 16 (over z, x_hi, core), space: 8 (over x_lo, y).
Axes of the slice: x: 4 (x_hi: 2, x_lo: 2; x = x_hi * 2 + x_lo), y: 4, z: 4, core: 2. Of those that a mesh axis runs over, the one named last changes fastest.
Arguments:
- solution: float32 [512, 384, 384], P('tm', 'space'), may hold values from -6 to 6
- residual: float32 [512, 384, 384], P('tm', 'space'), may hold values from -6 to 6
- direction: float32 [512, 384, 384], P('tm', 'space'), may hold values from -6 to 6
- reaction: float32 [512, 384, 384], P('tm', 'space'), may hold values from 0.1 to 2
- time_bands: float32 [2, 4, 512], replicated, may hold values from -0.25 to 1.1, as said below
- space_bands: float32 [2, 4, 384], replicated, may hold values from -0.25 to 1.1, as said below
- time_basis: float32 [512, 512], replicated, may hold values from -0.25 to 0.25
- space_basis: float32 [384, 384], replicated, may hold values from -0.3125 to 0.3125
- time_eigen: float32 [512], replicated, may hold values from 0.1 to 1
- space_eigen: float32 [384], replicated, may hold values from 0.1 to 1
Outputs:
- new_solution: float32 [512, 384, 384], P('tm', 'space')
- new_residual: float32 [512, 384, 384], P('tm', 'space')
- new_direction: float32 [512, 384, 384], P('tm', 'space')
Inputs may be any that keep to these rules, and one draw needn't show every extreme that they name: `time_bands`: each of the two matrices is symmetric with every diagonal entry larger than the sum of the magnitudes of the other entries of its row. `space_bands`: each of the two matrices is symmetric with every diagonal entry larger than the sum of the magnitudes of the other entries of its row.
All inputs are finite; a program needn't handle non-finite values.
Results may differ from a plain program's by a relative error of at most 0.000051.
Values sent between devices are 32-bit elements; how exact they have to be, the bound alone decides.
A program may use at most 128 MiB of HBM per device.

v0:
```python
import jax
import jax.numpy as jnp
from jax import lax
from jax.sharding import Mesh
from jax.sharding import PartitionSpec as P

TM_SPACE = ("tm_0", "tm_1", "tm_2", "space_0", "space_1")
TM = ("tm_0", "tm_1", "tm_2")
SPACE = ("space_0", "space_1")
highest = lax.Precision.HIGHEST


def extended_2(cells, sides, width):
    for axis, dim in sides:
        count = lax.axis_size(axis)
        ends = count - 1
        head = lax.slice_in_dim(cells, 0, width, axis=dim)
        tail = lax.slice_in_dim(cells, cells.shape[dim] - width, cells.shape[dim], axis=dim)
        cells = jnp.concatenate(
            [
                lax.ppermute(tail, axis, [(i, (i + 1) % count) for i in range(ends)]),
                cells,
                lax.ppermute(head, axis, [((i + 1) % count, i) for i in range(ends)]),
            ],
            axis=dim,
        )
    return cells


def cut_along(shard, dim, count):
    before, after = (shard.shape[:dim], shard.shape[dim + 1 :])
    return jnp.moveaxis(shard.reshape(*before, count, -1, *after), dim, 0)


def joined_along(pieces, dim):
    lengths = list(pieces.shape[1:])
    lengths[dim] *= pieces.shape[0]
    return jnp.moveaxis(pieces, 0, dim).reshape(lengths)


def exchange_in_order(pieces, axes, turns):
    lengths = [lax.axis_size(a) for a in axes]
    pieces = pieces.reshape(*lengths, *pieces.shape[1:])
    for k in turns:
        pieces = lax.all_to_all(pieces, axes[k], split_axis=k, concat_axis=k, tiled=True)
    return pieces.reshape(-1, *pieces.shape[len(axes) :])


def two_step_exchange(shard, groups, turns, split_dim, concat_dim):
    count = lax.axis_size(groups[0]) * lax.axis_size(groups[1])
    pieces = cut_along(shard, split_dim, count)
    return joined_along(exchange_in_order(pieces, groups, turns), concat_dim)


def over_axes(shard, axes):
    for axis in axes:
        shard = lax.psum(shard, axis)
    return shard


def band_apply(extended, band_rows, dimension):
    length = extended.shape[dimension] - 6
    target_shape = [1] * extended.ndim
    target_shape[dimension] = length

    def coefficient(which_row, first_row):
        return lax.slice_in_dim(band_rows[which_row], first_row, first_row + length).reshape(
            target_shape
        )

    def window(first_row):
        return lax.slice_in_dim(extended, first_row, first_row + length, axis=dimension)

    result = coefficient(0, 3) * window(3)
    for offset in (1, 2, 3):
        result = (
            result
            + coefficient(offset, 3) * window(3 + offset)
            + coefficient(offset, 3 - offset) * window(3 - offset)
        )
    return result


def pad_along(values, dimension):
    widths = [(0, 0)] * values.ndim
    widths[dimension] = (3, 3)
    return jnp.pad(values, widths)


def apply_operator(direction, reaction, time_bands, space_bands):
    rows_time = direction.shape[0]
    rows_space = direction.shape[1]
    halo_block = extended_2(direction, ((TM, 0), (SPACE, 1)), 3)
    padded_time = jnp.pad(time_bands, ((0, 0), (0, 0), (3, 3)))
    padded_space = jnp.pad(space_bands, ((0, 0), (0, 0), (3, 3)))
    time_rows = lax.dynamic_slice_in_dim(
        padded_time, lax.axis_index(TM) * rows_time, rows_time + 6, 2
    )
    space_rows = lax.dynamic_slice_in_dim(
        padded_space, lax.axis_index(SPACE) * rows_space, rows_space + 6, 2
    )
    extended = pad_along(halo_block, 2)
    mass_y = band_apply(extended, padded_space[1], 2)
    stiff_y = band_apply(extended, padded_space[0], 2)
    mass_xy = band_apply(mass_y, space_rows[1], 1)
    stiff_x = band_apply(mass_y, space_rows[0], 1)
    stiff_yx = band_apply(stiff_y, space_rows[1], 1)
    temporal = band_apply(mass_xy, time_rows[0], 0) + band_apply(
        stiff_x + stiff_yx, time_rows[1], 0
    )
    return temporal + reaction * direction


def spectrum(time_eigen, space_eigen):
    time_count = lax.axis_size(TM)
    space_count = lax.axis_size(SPACE)
    block_width = space_eigen.shape[0] // (time_count * space_count)
    group_index = lax.axis_index(SPACE) * time_count + lax.axis_index(TM)
    block = lax.dynamic_slice_in_dim(space_eigen, group_index * block_width, block_width)
    return time_eigen[:, None, None] + space_eigen[None, :, None] + block[None, None, :]


def forward_fields(fields, time_basis, space_basis):
    along_y = jnp.einsum("ctxk,ka->ctxa", fields, space_basis, precision=highest)
    spread = lax.all_to_all(along_y, SPACE, split_axis=3, concat_axis=2, tiled=True)
    along_x = jnp.einsum("ctjy,jb->ctby", spread, space_basis, precision=highest)
    joined = lax.all_to_all(along_x, TM, split_axis=3, concat_axis=1, tiled=True)
    return jnp.einsum("cixy,ia->caxy", joined, time_basis, precision=highest)


def inverse_fields(spectral, time_basis, space_basis):
    along_t = jnp.einsum("caxy,ia->cixy", spectral, time_basis, precision=highest)
    parted = two_step_exchange(along_t, (("tm_0", "tm_1"), "tm_2"), (1, 0), 1, 3)
    along_x = jnp.einsum("ctby,jb->ctjy", parted, space_basis, precision=highest)
    blocks = lax.all_to_all(along_x, SPACE, split_axis=2, concat_axis=3, tiled=True)
    return jnp.einsum("ctxa,ka->ctxk", blocks, space_basis, precision=highest)


def per_device(
    solution,
    residual,
    direction,
    reaction,
    time_bands,
    space_bands,
    time_basis,
    space_basis,
    time_eigen,
    space_eigen,
):
    image = apply_operator(direction, reaction, time_bands, space_bands)
    eigen_sum = spectrum(time_eigen, space_eigen)
    both_hat = forward_fields(jnp.stack([residual, image]), time_basis, space_basis)
    first_scaled = both_hat[0] / eigen_sum
    image_scaled = both_hat[1] / eigen_sum
    norm_old, cross_term, image_norm, curvature = (
        over_axes(jnp.sum(both_hat[0] * first_scaled), TM_SPACE),
        over_axes(jnp.sum(both_hat[1] * first_scaled), TM_SPACE),
        over_axes(jnp.sum(both_hat[1] * image_scaled), TM_SPACE),
        over_axes(jnp.sum(direction * image), TM_SPACE),
    )
    step_size = norm_old / curvature
    new_residual = residual - step_size * image
    spectral = first_scaled - step_size * image_scaled
    norm_new = norm_old - 2.0 * step_size * cross_term + step_size * step_size * image_norm
    precond = inverse_fields(spectral[None], time_basis, space_basis)[0]
    new_direction = precond + norm_new / norm_old * direction
    new_solution = solution + step_size * direction
    return (new_solution, new_residual, new_direction)


def solution(mesh):
    finer = Mesh(
        mesh.devices.reshape(4, 2, 2, 2, 4), ("tm_0", "tm_1", "tm_2", "space_0", "space_1")
    )
    in_specs = (
        P(TM, SPACE, None),
        P(TM, SPACE, None),
        P(TM, SPACE, None),
        P(TM, SPACE, None),
        P(),
        P(),
        P(),
        P(),
        P(),
        P(),
    )
    out_specs = (P(TM, SPACE, None), P(TM, SPACE, None), P(TM, SPACE, None))
    return jax.shard_map(
        per_device, mesh=finer, in_specs=in_specs, out_specs=out_specs, check_vma=False
    )
```

profile of v0, /device:TPU:1, one launch (start us, length us, event | category | flops | bytes accessed | tf_op | source)
XLA Modules:
  0.0 526.5 jit_solution(127195260726409566)
XLA Ops:
  1.8 6.0 %collective-permute-start = (f32[3,48,384]{2,1,0:T(8,128)S(1)}, f32[3,48,384]{2,1,0:T(8,128)S(1)}, u32[]{:S(2)}, u32[]{:S(2)}) collective-permute-start(f32[3,48,384]{2,1,0:T(8,128)S(1)} %get-tuple-element.47), channel_id=1, source_target_pairs={{0,8},{8,16},{16,24},{24,32},{32,40},{40,48},{48,56},{56,64},{64,7... | collective-permute-start | bytes 663560 | tf_op jit(solution)/shard_map/ppermute | solution.py:21
  28.8 30.2 %multiply_add_fusion.1 = (f32[38,54,384]{2,1,0:T(8,128)}, f32[38,54,384]{2,1,0:T(8,128)}) fusion(f32[38,54,384]{2,1,0:T(8,128)} %pad_maximum_fusion, f32[384]{0:T(512)S(1)} %get-tuple-element.9, f32[384]{0:T(512)S(1)} %get-tuple-element.15, f32[384]{0:T(512)S(1)} %get-tuple-element.8, f32[384]{0:T(512)S(1)} %get-tuple-element.16, ...), kind=kLoop, calls=%fused_computation.18 | loop fusion | flops 20487168 | bytes 9477120 | tf_op jit(solution)/shard_map/add | solution.py:77
  59.0 12.2 %multiply_add_fusion.2 = f32[38,48,384]{2,1,0:T(8,128)} fusion(f32[38,54,384]{2,1,0:T(8,128)} %get-tuple-element.42, f32[48]{0:T(128)S(1)} %get-tuple-element.70, f32[48]{0:T(128)S(1)} %get-tuple-element.71, f32[48]{0:T(128)S(1)} %get-tuple-element.72, f32[48]{0:T(128)S(1)} %get-tuple-element.73, f32[48]{0:T(128)S(1)} %get-tuple-element.75, ...), kind=kLoop, calls=%fused_computation.33 | loop fusion | flops 9105408 | bytes 22414656 | tf_op jit(solution)/shard_map/add | solution.py:77
  77.1 16.6 %multiply_reduce_fusion = (f32[]{:T(128)}, f32[32,48,384]{2,1,0:T(8,128)S(1)}) fusion(f32[32,48,384]{2,1,0:T(8,128)} %param.12, f32[32,48,384]{2,1,0:T(8,128)} %param.13, f32[38,48,384]{2,1,0:T(8,128)} %fusion.5, f32[32]{0:T(128)S(1)} %get-tuple-element.54, f32[32]{0:T(128)S(1)} %get-tuple-element.55, f32[32]{0:T(128)S(1)} %get-tuple-element.53, ...), kind=kLoop, calls=%fused_computation.75 | loop fusion | flops 18284544 | bytes 40109828 | tf_op jit(solution)/shard_map/reduce_sum | solution.py:160
  95.1 10.6 %fusion = f32[2,32,48,384]{3,2,1,0:T(8,128)} fusion(f32[1,32,48,384]{3,2,1,0:T(8,128)S(1)} %bitcast.155, f32[1,32,48,384]{3,2,1,0:T(8,128)S(1)} %bitcast.157, f32[384,384]{1,0:T(8,128)S(1)} %copy-done.7), kind=kOutput, calls=%fused_computation.8 | convolution fusion | flops 5436997632 | bytes 10027008 | tf_op jit(solution)/shard_map/ctxk,ka->ctxa/dot_general | solution.py:124
  105.7 12.0 %copy.26 = f32[2,32,48,384]{2,1,0,3:T(8,128)} copy(f32[2,32,48,384]{3,2,1,0:T(8,128)} %fusion) | data formatting | bytes 9437184 | tf_op jit(solution)/shard_map/ctxk,ka->ctxa/dot_general | solution.py:124
  117.8 14.4 %reshape.301 = f32[8,1,147456]{2,1,0:T(1,128)} reshape(f32[384,2,32,48]{3,2,1,0:T(8,128)} %bitcast.151) | data formatting | bytes 9437184
  132.2 57.9 %all_to_all.61 = f32[8,1,147456]{2,1,0:T(1,128)} all-to-all(f32[8,1,147456]{2,1,0:T(1,128)} %reshape.301), channel_id=1, replica_groups=mesh['tm_0'=4,'tm_1'=2,'tm_2'=2,'space_0'=2,'space_1'=4] {'space_0','spa..., dimensions={0} | all-to-all | bytes 9437184 | tf_op jit(solution)/shard_map/all_to_all | solution.py:125
  190.5 15.9 %reduce.28 = f32[8,147456]{1,0:T(8,128)} reduce(f32[8,1,147456]{2,1,0:T(1,128)} %all_to_all.61, f32[]{:T(128)} %broadcast.59), dimensions={1}, to_apply=%all_to_all.43.reduce_sub_computation | reduce | bytes 9437188 | tf_op jit(solution)/shard_map/all_to_all | solution.py:125
  206.4 11.9 %reshape.302 = f32[384,2,32,48]{3,2,1,0:T(8,128)} reshape(f32[8,147456]{1,0:T(8,128)} %reduce.28) | data formatting | bytes 9437184
  218.4 16.7 %copy.52 = f32[2,32,48,8,48]{2,3,4,1,0:T(8,128)} copy(f32[2,32,48,8,48]{2,1,0,4,3:T(8,128)} %bitcast.149) | data formatting | bytes 9437184 | tf_op jit(solution)/shard_map/all_to_all | solution.py:125
  235.1 10.7 %all_to_all.46 = f32[2,32,384,48]{2,3,1,0:T(8,128)} reshape(f32[2,32,8,48,48]{3,2,4,1,0:T(8,128)} %bitcast.150) | data formatting | bytes 9437184 | tf_op jit(solution)/shard_map/all_to_all | solution.py:125
  245.8 11.8 %convolution_bitcast_fusion = f32[2,32,384,48]{2,3,1,0:T(8,128)S(1)} fusion(f32[2,32,384,48]{2,3,1,0:T(8,128)} %all_to_all.46, f32[384,384]{1,0:T(8,128)S(1)} %copy-done.7), kind=kOutput, calls=%fused_computation.77 | convolution fusion | flops 5435817984 | bytes 10027008 | tf_op jit(solution)/shard_map/ctjy,jb->ctby/dot_general | solution.py:126
  261.2 13.3 %all-to-all-start.1 = ((f32[2,32,384,48]{2,1,0,3:T(8,128)}), f32[2,32,384,48]{2,1,0,3:T(8,128)}, u32[]{:S(2)}, u32[]{:S(2)}) async-start(f32[2,32,384,48]{2,1,0,3:T(8,128)} %copy.28), calls=%async_computation.1 | async-start | bytes 9437184 | tf_op jit(solution)/shard_map/all_to_all | solution.py:127
  274.7 56.2 %all-to-all-done.1 = f32[2,32,384,48]{2,1,0,3:T(8,128)} async-done(((f32[2,32,384,48]{2,1,0,3:T(8,128)}), f32[2,32,384,48]{2,1,0,3:T(8,128)}, u32[]{:S(2)}, u32[]{:S(2)}) %all-to-all-start.1) | async-done | bytes 4718624 | tf_op jit(solution)/shard_map/all_to_all | solution.py:127
  333.7 8.0 %convolution_bitcast_fusion.1 = f32[2,512,384,3]{1,2,3,0:T(8,128)S(1)} fusion(f32[2,512,384,3]{2,1,3,0:T(8,128)S(1)} %bitcast.156, f32[512,512]{1,0:T(8,128)S(1)} %copy-done), kind=kOutput, calls=%fused_computation.78 | convolution fusion | flops 7247757312 | bytes 10485760 | tf_op jit(solution)/shard_map/cixy,ia->caxy/dot_general | solution.py:128
  346.0 7.9 %all-reduce.4 = (f32[]{:T(128)}, f32[]{:T(128)}, f32[]{:T(128)}, f32[]{:T(128)}) all-reduce(f32[]{:T(128)} %get-tuple-element.5, f32[]{:T(128)} %get-tuple-element.40, f32[]{:T(128)} %get-tuple-element.4, f32[]{:T(128)} %get-tuple-element.3), channel_id=1, replica_groups=mesh['tm_0'=4,'tm_1'=2,'tm_2'=2,'space_0'=2,'space_1'=4] {'tm_0'}, use_global_device_ids=true, to_apply=%region_1.2 | all-reduce | flops 4 | bytes 32 | tf_op jit(solution)/shard_map/psum | solution.py:57
  353.9 6.0 %all-reduce.7 = (f32[]{:T(128)}, f32[]{:T(128)}, f32[]{:T(128)}, f32[]{:T(128)}) all-reduce(f32[]{:T(128)} %get-tuple-element.24, f32[]{:T(128)} %get-tuple-element.25, f32[]{:T(128)} %get-tuple-element.26, f32[]{:T(128)} %get-tuple-element.27), channel_id=1, replica_groups=mesh['tm_0'=4,'tm_1'=2,'tm_2'=2,'space_0'=2,'space_1'=4] {'tm_1'}, use_global_device_ids=true, to_apply=%region_2.3 | all-reduce | flops 4 | bytes 32 | tf_op jit(solution)/shard_map/psum | solution.py:57
  359.9 7.0 %all-reduce.6 = (f32[]{:T(128)}, f32[]{:T(128)}, f32[]{:T(128)}, f32[]{:T(128)}) all-reduce(f32[]{:T(128)} %get-tuple-element.36, f32[]{:T(128)} %get-tuple-element.37, f32[]{:T(128)} %get-tuple-element.38, f32[]{:T(128)} %get-tuple-element.39), channel_id=1, replica_groups=mesh['tm_0'=4,'tm_1'=2,'tm_2'=2,'space_0'=2,'space_1'=4] {'tm_2'}, use_global_device_ids=true, to_apply=%region_3.4 | all-reduce | flops 4 | bytes 32 | tf_op jit(solution)/shard_map/psum | solution.py:57
  371.4 7.6 %all-reduce.3 = (f32[]{:T(128)}, f32[]{:T(128)}, f32[]{:T(128)}, f32[]{:T(128)}) all-reduce(f32[]{:T(128)} %get-tuple-element.28, f32[]{:T(128)} %get-tuple-element.29, f32[]{:T(128)} %get-tuple-element.30, f32[]{:T(128)} %get-tuple-element.31), channel_id=1, replica_groups=mesh['tm_0'=4,'tm_1'=2,'tm_2'=2,'space_0'=2,'space_1'=4] {'space_1'}, use_global_device_ids=true, to_apply=%region_5.6 | all-reduce | flops 4 | bytes 32 | tf_op jit(solution)/shard_map/psum | solution.py:57
  380.3 7.2 %fusion.38 = f32[8,2,1,32,384,3]{4,3,1,0,5,2:T(8,128)S(1)} fusion(f32[8,2,32,512,1]{3,2,1,0,4:T(8,128)S(1)} %bitcast.148, f32[2,512,384,3]{1,2,3,0:T(8,128)} %copy-done.5, f32[]{:T(128)S(6)} %div.19, f32[3]{0:T(128)S(1)} %dynamic_slice.11, f32[512,384]{0,1:T(8,128)S(1)} %broadcast_add_fusion), kind=kOutput, calls=%fused_computation.81 | convolution fusion | flops 3626827776 | bytes 8912912 | tf_op jit(solution)/shard_map/caxy,ia->cixy/dot_general | solution.py:132
  387.7 8.8 %all_to_all.62 = f32[8,2,1,32,384,3]{4,3,0,5,2,1:T(8,128)S(1)} all-to-all(f32[8,2,1,32,384,3]{4,3,0,5,2,1:T(8,128)S(1)} %copy.33), channel_id=1, replica_groups=mesh['tm_0'=4,'tm_1'=2,'tm_2'=2,'space_0'=2,'space_1'=4] {'tm_2'}, dimensions={1} | all-to-all | bytes 4718592 | tf_op jit(solution)/shard_map/all_to_all | solution.py:45
  396.7 33.4 %all_to_all.63 = f32[8,2,1,32,384,3]{4,3,1,5,2,0:T(8,128)S(1)} all-to-all(f32[8,2,1,32,384,3]{4,3,1,5,2,0:T(8,128)S(1)} %copy.34), channel_id=1, replica_groups=mesh['tm_0'=4,'tm_1'=2,'tm_2'=2,'space_0'=2,'space_1'=4] {'tm_0','tm_1'}, dimensions={0} | all-to-all | bytes 4718592 | tf_op jit(solution)/shard_map/all_to_all | solution.py:45
  430.3 7.2 %fusion.41 = f32[1,32,384,48]{2,3,1,0:T(8,128)} fusion(f32[32,384,48]{1,0,2:T(8,128)S(1)} %bitcast.158, f32[384,384]{1,0:T(8,128)S(1)} %copy-done.7), kind=kOutput, calls=%fused_computation.82 | convolution fusion | flops 2717908992 | bytes 5308416 | tf_op jit(solution)/shard_map/ctby,jb->ctjy/dot_general | solution.py:134
  437.5 7.2 %copy.37 = f32[1,32,384,48]{3,1,0,2:T(8,128)} copy(f32[1,32,384,48]{2,3,1,0:T(8,128)} %fusion.41) | data formatting | bytes 4718592 | tf_op jit(solution)/shard_map/ctby,jb->ctjy/transpose | solution.py:134
  444.7 9.5 %reshape.303 = f32[8,1,73728]{2,1,0:T(1,128)} reshape(f32[384,1,32,48]{3,2,1,0:T(8,128)} %bitcast.154) | data formatting | bytes 4718592
  467.2 20.5 %all-to-all-done.4 = f32[8,1,73728]{2,1,0:T(1,128)} async-done(((f32[8,1,73728]{2,1,0:T(1,128)}), f32[8,1,73728]{2,1,0:T(1,128)}, u32[]{:S(2)}, u32[]{:S(2)}) %all-to-all-start.4) | async-done | bytes 2359328 | tf_op jit(solution)/shard_map/all_to_all | solution.py:135
  487.7 9.3 %reduce.29 = f32[8,73728]{1,0:T(8,128)} reduce(f32[8,1,73728]{2,1,0:T(1,128)} %all-to-all-done.4, f32[]{:T(128)} %broadcast.59), dimensions={1}, to_apply=%all_to_all.53.reduce_sub_computation | reduce | bytes 4718596 | tf_op jit(solution)/shard_map/all_to_all | solution.py:135
  497.0 6.9 %reshape.304 = f32[384,1,32,48]{3,2,1,0:T(8,128)} reshape(f32[8,73728]{1,0:T(8,128)} %reduce.29) | data formatting | bytes 4718592
  503.9 9.3 %copy.53 = f32[1,32,8,48,48]{4,2,3,1,0:T(8,128)} copy(f32[1,32,8,48,48]{4,1,3,2,0:T(8,128)} %bitcast.152) | data formatting | bytes 4718592 | tf_op jit(solution)/shard_map/all_to_all | solution.py:135
  513.2 5.9 %reshape.281 = f32[32,48,384]{2,1,0:T(8,128)} reshape(f32[1,32,48,8,48]{4,3,2,1,0:T(8,128)} %bitcast.153) | data formatting | bytes 4718592 | tf_op jit(solution)/shard_map/reshape.193
  519.1 7.2 %multiply_add_fusion.3 = f32[32,48,384]{2,1,0:T(8,128)} fusion(f32[32,48,384]{2,1,0:T(8,128)S(1)} %copy-done.3, f32[32,48,384]{2,1,0:T(8,128)} %reshape.281, f32[]{:T(128)S(6)} %div.23, f32[384,384]{1,0:T(8,128)} %param.17), kind=kOutput, calls=%fused_computation.72 | convolution fusion | flops 2719088640 | bytes 7667716 | tf_op jit(solution)/shard_map/ctxa,ka->ctxk/dot_general | solution.py:136
  (55 shorter events, 56.3 us)
Async XLA Ops:
  0.6 333.0 %copy-start = (f32[512,512]{1,0:T(8,128)S(1)}, f32[512,512]{1,0:T(8,128)}, u32[]{:S(2)}) copy-start(f32[512,512]{1,0:T(8,128)} %param.16) | copy-start | bytes 3145732
  1.8 11.0 %collective-permute-start = (f32[3,48,384]{2,1,0:T(8,128)S(1)}, f32[3,48,384]{2,1,0:T(8,128)S(1)}, u32[]{:S(2)}, u32[]{:S(2)}) collective-permute-start(f32[3,48,384]{2,1,0:T(8,128)S(1)} %get-tuple-element.47), channel_id=1, source_target_pairs={{0,8},{8,16},{16,24},{24,32},{32,40},{40,48},{48,56},{56,64},{64,7... | collective-permute-start | bytes 663560 | tf_op jit(solution)/shard_map/ppermute | solution.py:21
  7.8 8.8 %collective-permute-start.1 = (f32[3,48,384]{2,1,0:T(8,128)S(1)}, f32[3,48,384]{2,1,0:T(8,128)S(1)}, u32[]{:S(2)}, u32[]{:S(2)}) collective-permute-start(f32[3,48,384]{2,1,0:T(8,128)S(1)} %get-tuple-element.46), channel_id=1, source_target_pairs={{8,0},{16,8},{24,16},{32,24},{40,32},{48,40},{56,48},{64,56},{72,6... | collective-permute-start | bytes 663560 | tf_op jit(solution)/shard_map/ppermute | solution.py:23
  12.8 8.4 %copy-start.9 = (f32[2,4,512]{2,1,0:T(4,128)S(1)}, f32[2,4,512]{2,1,0:T(4,128)}, u32[]{:S(2)}) copy-start(f32[2,4,512]{2,1,0:T(4,128)} %param.14) | copy-start | bytes 49156
  12.8 8.5 %copy-start.8 = (f32[2,4,384]{2,1,0:T(4,128)S(1)}, f32[2,4,384]{2,1,0:T(4,128)}, u32[]{:S(2)}) copy-start(f32[2,4,384]{2,1,0:T(4,128)} %param.15) | copy-start | bytes 36868
  16.7 6.2 %collective-permute-start.2 = (f32[38,3,384]{2,1,0:T(4,128)S(1)}, f32[38,3,384]{2,1,0:T(4,128)S(1)}, u32[]{:S(2)}, u32[]{:S(2)}) collective-permute-start(f32[38,3,384]{2,1,0:T(4,128)S(1)} %get-tuple-element.44), channel_id=1, source_target_pairs={{0,1},{1,2},{2,3},{3,4},{4,5},{5,6},{6,7},{8,9},{9,10},{10,11},{11... | collective-permute-start | bytes 525320 | tf_op jit(solution)/shard_map/ppermute | solution.py:21
  19.9 6.8 %collective-permute-start.3 = (f32[38,3,384]{2,1,0:T(4,128)S(1)}, f32[38,3,384]{2,1,0:T(4,128)S(1)}, u32[]{:S(2)}, u32[]{:S(2)}) collective-permute-start(f32[38,3,384]{2,1,0:T(4,128)S(1)} %get-tuple-element.45), channel_id=1, source_target_pairs={{1,0},{2,1},{3,2},{4,3},{5,4},{6,5},{7,6},{9,8},{10,9},{11,10},{12... | collective-permute-start | bytes 525320 | tf_op jit(solution)/shard_map/ppermute | solution.py:23
  59.0 12.2 %copy-start.1 = (f32[38,54,384]{2,1,0:T(8,128)S(1)}, f32[38,54,384]{2,1,0:T(8,128)}, u32[]{:S(2)}) copy-start(f32[38,54,384]{2,1,0:T(8,128)} %get-tuple-element.42) | copy-start | bytes 9455620
  59.0 12.2 %copy-start.2 = (f32[38,54,384]{2,1,0:T(8,128)S(1)}, f32[38,54,384]{2,1,0:T(8,128)}, u32[]{:S(2)}) copy-start(f32[38,54,384]{2,1,0:T(8,128)} %get-tuple-element.43) | copy-start | bytes 9455620
  77.1 18.0 %copy-start.6 = (f32[32,48,384]{2,1,0:T(8,128)S(1)}, f32[32,48,384]{2,1,0:T(8,128)}, u32[]{:S(2)}) copy-start(f32[32,48,384]{2,1,0:T(8,128)} %param.11) | copy-start | bytes 7077892
  77.1 18.0 %copy-start.7 = (f32[384,384]{1,0:T(8,128)S(1)}, f32[384,384]{1,0:T(8,128)}, u32[]{:S(2)}) copy-start(f32[384,384]{1,0:T(8,128)} %param.17) | copy-start | bytes 1769476
  93.7 1.4 copy-start.4
  261.2 13.3 %copy-start.10 = (f32[384]{0:T(512)S(1)}, f32[384]{0:T(512)}, u32[]{:S(2)}) copy-start(f32[384]{0:T(512)} %param.19) | copy-start | bytes 4612
  261.2 13.4 %copy-start.11 = (f32[512]{0:T(512)S(1)}, f32[512]{0:T(512)}, u32[]{:S(2)}) copy-start(f32[512]{0:T(512)} %param.18) | copy-start | bytes 6148
  261.2 69.7 %all-to-all-start.1 = ((f32[2,32,384,48]{2,1,0,3:T(8,128)}), f32[2,32,384,48]{2,1,0,3:T(8,128)}, u32[]{:S(2)}, u32[]{:S(2)}) async-start(f32[2,32,384,48]{2,1,0,3:T(8,128)} %copy.28), calls=%async_computation.1 | async-start | bytes 9437184 | tf_op jit(solution)/shard_map/all_to_all | solution.py:127
  341.7 2.1 copy-start.5
  454.2 7.2 %copy-start.3 = (f32[32,48,384]{2,1,0:T(8,128)S(1)}, f32[32,48,384]{2,1,0:T(8,128)}, u32[]{:S(2)}) copy-start(f32[32,48,384]{2,1,0:T(8,128)} %param.12) | copy-start | bytes 7077892
  454.2 33.5 %all-to-all-start.4 = ((f32[8,1,73728]{2,1,0:T(1,128)}), f32[8,1,73728]{2,1,0:T(1,128)}, u32[]{:S(2)}, u32[]{:S(2)}) async-start(f32[8,1,73728]{2,1,0:T(1,128)} %reshape.303), calls=%async_computation.4 | async-start | bytes 4718592 | tf_op jit(solution)/shard_map/all_to_all | solution.py:135
where the time goes:
time: 537 us; the launch traced here: 526 us
  blocking collectives  133 us (25%)
  local copies, waits for them, and re-layouts  122 us (23%)
  other arithmetic  100 us (19%)
  waiting for transfers between devices  83.9 us (16%)
  matrix products  52 us (10%)
  starting transfers between devices  30.4 us (6%)
    all_to_all x1, blocking collectives, forward_fields(): lax.all_to_all(along_y, SPACE, split_axis=3, concat_axis=2, tiled=True)  57.9 us
    all_to_all x1, waiting for transfers between devices, forward_fields(): lax.all_to_all(along_x, TM, split_axis=3, concat_axis=1, tiled=True)  56.2 us
    unnamed x30, local copies, waits for them, and re-layouts  48.1 us
    add x2, other arithmetic, band_apply(): result + coefficient(offset, 3) * window(3 + offset)  42.4 us
    all_to_all x2, blocking collectives, exchange_in_order(): lax.all_to_all(pieces, axes[k], split_axis=k, concat_axis=k, tiled=True)  42.2 us
    psum x5, blocking collectives, over_axes(): shard = lax.psum(shard, axis)  33 us
    all_to_all x3, local copies, waits for them, and re-layouts, forward_fields(): lax.all_to_all(along_y, SPACE, split_axis=3, concat_axis=2, tiled=True)  27.9 us
    all_to_all x1, waiting for transfers between devices, inverse_fields(): lax.all_to_all(along_x, SPACE, split_axis=2, concat_axis=3, tiled=True)  20.5 us
  transfers between devices with their start and end apart: 6, of which 5 were waited for; matrix products, arithmetic and copies ran while one was open for 2% of the time, Pallas kernels for 0%

commit v1 on v0

--- a/solution.py
+++ b/solution.py
@@ -54,7 +54,7 @@
 
 def over_axes(shard, axes):
     for axis in axes:
-        shard = lax.psum(shard, axis)
+        shard = jnp.sum(lax.all_gather(shard, axis), axis=0)
     return shard
 
 

time: 537 us -> 573 us (1.067)
  local copies, waits for them, and re-layouts: 122 us -> 153 us
  other arithmetic: 100 us -> 112 us
    psum x5 -> x0, blocking collectives: 33 us -> none  [over_axes(): shard = lax.psum(shard, axis)]
    unnamed x30 -> x85, local copies, waits for them, and re-layouts: 48.1 us -> 78.9 us
    unnamed x0 -> x5, blocking collectives: none -> 29.1 us
    reduce_sum x0 -> x20, other arithmetic: none -> 11.9 us  [over_axes(): shard = jnp.sum(lax.all_gather(shard, axis), axis=0)]
  transfers between devices with their start and end apart: 6 -> 6, of which waited for: 5 -> 5; matrix products, arithmetic and copies ran while one was open for 2% -> 3% of each run, Pallas kernels for 0% -> 0%
where the time goes in v1:
time: 573 us; the launch traced here: 562 us
  local copies, waits for them, and re-layouts  153 us (27%)
  blocking collectives  130 us (23%)
  other arithmetic  112 us (20%)
  waiting for transfers between devices  80.5 us (14%)
  matrix products  52 us (9%)
  starting transfers between devices  30.1 us (5%)
    unnamed x85, local copies, waits for them, and re-layouts  78.9 us
    all_to_all x1, blocking collectives, forward_fields(): lax.all_to_all(along_y, SPACE, split_axis=3, concat_axis=2, tiled=True)  57.9 us
    all_to_all x1, waiting for transfers between devices, forward_fields(): lax.all_to_all(along_x, TM, split_axis=3, concat_axis=1, tiled=True)  54.1 us
    all_to_all x2, blocking collectives, exchange_in_order(): lax.all_to_all(pieces, axes[k], split_axis=k, concat_axis=k, tiled=True)  42.6 us
    add x2, other arithmetic, band_apply(): result + coefficient(offset, 3) * window(3 + offset)  42.4 us
    unnamed x5, blocking collectives  29.1 us
    all_to_all x3, local copies, waits for them, and re-layouts, forward_fields(): lax.all_to_all(along_y, SPACE, split_axis=3, concat_axis=2, tiled=True)  27.9 us
    all_to_all x1, waiting for transfers between devices, inverse_fields(): lax.all_to_all(along_x, SPACE, split_axis=2, concat_axis=3, tiled=True)  19.1 us
  transfers between devices with their start and end apart: 6, of which 5 were waited for; matrix products, arithmetic and copies ran while one was open for 3% of the time, Pallas kernels for 0%

profile of v1, /device:TPU:1, one launch (start us, length us, event | category | flops | bytes accessed | tf_op | source)
XLA Modules:
  0.0 562.2 jit_solution(1704680860621568538)
XLA Ops:
  1.8 6.0 %collective-permute-start = (f32[3,48,384]{2,1,0:T(8,128)S(1)}, f32[3,48,384]{2,1,0:T(8,128)S(1)}, u32[]{:S(2)}, u32[]{:S(2)}) collective-permute-start(f32[3,48,384]{2,1,0:T(8,128)S(1)} %get-tuple-element.47), channel_id=1, source_target_pairs={{0,8},{8,16},{16,24},{24,32},{32,40},{40,48},{48,56},{56,64},{64,7... | collective-permute-start | bytes 663560 | tf_op jit(solution)/shard_map/ppermute | solution.py:21
  28.8 30.2 %multiply_add_fusion.1 = (f32[38,54,384]{2,1,0:T(8,128)}, f32[38,54,384]{2,1,0:T(8,128)}) fusion(f32[38,54,384]{2,1,0:T(8,128)} %pad_maximum_fusion, f32[384]{0:T(512)S(1)} %get-tuple-element.9, f32[384]{0:T(512)S(1)} %get-tuple-element.15, f32[384]{0:T(512)S(1)} %get-tuple-element.8, f32[384]{0:T(512)S(1)} %get-tuple-element.16, ...), kind=kLoop, calls=%fused_computation.18 | loop fusion | flops 20487168 | bytes 9477120 | tf_op jit(solution)/shard_map/add | solution.py:77
  59.0 12.2 %multiply_add_fusion.2 = f32[38,48,384]{2,1,0:T(8,128)} fusion(f32[38,54,384]{2,1,0:T(8,128)} %get-tuple-element.42, f32[48]{0:T(128)S(1)} %get-tuple-element.70, f32[48]{0:T(128)S(1)} %get-tuple-element.71, f32[48]{0:T(128)S(1)} %get-tuple-element.72, f32[48]{0:T(128)S(1)} %get-tuple-element.73, f32[48]{0:T(128)S(1)} %get-tuple-element.75, ...), kind=kLoop, calls=%fused_computation.33 | loop fusion | flops 9105408 | bytes 22414656 | tf_op jit(solution)/shard_map/add | solution.py:77
  71.2 5.8 %fusion.5 = f32[38,48,384]{2,1,0:T(8,128)} fusion(f32[38,54,384]{2,1,0:T(8,128)S(1)} %copy-done.2, f32[38,54,384]{2,1,0:T(8,128)S(1)} %copy-done.1, f32[48]{0:T(128)S(1)} %get-tuple-element.64, f32[48]{0:T(128)S(1)} %get-tuple-element.65, f32[48]{0:T(128)S(1)} %get-tuple-element.63, f32[48]{0:T(128)S(1)} %get-tuple-element.66, f32[48]{0:T(128)S(1)} %get-tuple-element.68, ...), kind=kLoop, calls=%fused_computation.21 | loop fusion | flops 18911232 | bytes 42027648 | tf_op jit(solution)/shard_map/add | solution.py:109
  77.1 16.6 %multiply_reduce_fusion = (f32[]{:T(128)}, f32[32,48,384]{2,1,0:T(8,128)S(1)}) fusion(f32[32,48,384]{2,1,0:T(8,128)} %param.12, f32[32,48,384]{2,1,0:T(8,128)} %param.13, f32[38,48,384]{2,1,0:T(8,128)} %fusion.5, f32[32]{0:T(128)S(1)} %get-tuple-element.54, f32[32]{0:T(128)S(1)} %get-tuple-element.55, f32[32]{0:T(128)S(1)} %get-tuple-element.53, ...), kind=kLoop, calls=%fused_computation.75 | loop fusion | flops 18284544 | bytes 40109828 | tf_op jit(solution)/shard_map/reduce_sum | solution.py:160
  95.1 10.6 %fusion = f32[2,32,48,384]{3,2,1,0:T(8,128)} fusion(f32[1,32,48,384]{3,2,1,0:T(8,128)S(1)} %bitcast.180, f32[1,32,48,384]{3,2,1,0:T(8,128)S(1)} %bitcast.182, f32[384,384]{1,0:T(8,128)S(1)} %copy-done.7), kind=kOutput, calls=%fused_computation.8 | convolution fusion | flops 5436997632 | bytes 10027008 | tf_op jit(solution)/shard_map/ctxk,ka->ctxa/dot_general | solution.py:124
  105.7 12.0 %copy.26 = f32[2,32,48,384]{2,1,0,3:T(8,128)} copy(f32[2,32,48,384]{3,2,1,0:T(8,128)} %fusion) | data formatting | bytes 9437184 | tf_op jit(solution)/shard_map/ctxk,ka->ctxa/dot_general | solution.py:124
  117.8 14.4 %reshape.401 = f32[8,1,147456]{2,1,0:T(1,128)} reshape(f32[384,2,32,48]{3,2,1,0:T(8,128)} %bitcast.176) | data formatting | bytes 9437184
  132.2 57.9 %all_to_all.61 = f32[8,1,147456]{2,1,0:T(1,128)} all-to-all(f32[8,1,147456]{2,1,0:T(1,128)} %reshape.401), channel_id=1, replica_groups=mesh['tm_0'=4,'tm_1'=2,'tm_2'=2,'space_0'=2,'space_1'=4] {'space_0','spa..., dimensions={0} | all-to-all | bytes 9437184 | tf_op jit(solution)/shard_map/all_to_all | solution.py:125
  190.6 15.9 %reduce.48 = f32[8,147456]{1,0:T(8,128)} reduce(f32[8,1,147456]{2,1,0:T(1,128)} %all_to_all.61, f32[]{:T(128)} %broadcast.79), dimensions={1}, to_apply=%all_to_all.43.reduce_sub_computation | reduce | bytes 9437188 | tf_op jit(solution)/shard_map/all_to_all | solution.py:125
  206.4 11.9 %reshape.402 = f32[384,2,32,48]{3,2,1,0:T(8,128)} reshape(f32[8,147456]{1,0:T(8,128)} %reduce.48) | data formatting | bytes 9437184
  218.4 16.7 %copy.52 = f32[2,32,48,8,48]{2,3,4,1,0:T(8,128)} copy(f32[2,32,48,8,48]{2,1,0,4,3:T(8,128)} %bitcast.174) | data formatting | bytes 9437184 | tf_op jit(solution)/shard_map/all_to_all | solution.py:125
  235.1 10.7 %all_to_all.46 = f32[2,32,384,48]{2,3,1,0:T(8,128)} reshape(f32[2,32,8,48,48]{3,2,4,1,0:T(8,128)} %bitcast.175) | data formatting | bytes 9437184 | tf_op jit(solution)/shard_map/all_to_all | solution.py:125
  245.8 11.8 %convolution_bitcast_fusion = f32[2,32,384,48]{2,3,1,0:T(8,128)S(1)} fusion(f32[2,32,384,48]{2,3,1,0:T(8,128)} %all_to_all.46, f32[384,384]{1,0:T(8,128)S(1)} %copy-done.7), kind=kOutput, calls=%fused_computation.77 | convolution fusion | flops 5435817984 | bytes 10027008 | tf_op jit(solution)/shard_map/ctjy,jb->ctby/dot_general | solution.py:126
  261.2 12.9 %all-to-all-start.1 = ((f32[2,32,384,48]{2,1,0,3:T(8,128)}), f32[2,32,384,48]{2,1,0,3:T(8,128)}, u32[]{:S(2)}, u32[]{:S(2)}) async-start(f32[2,32,384,48]{2,1,0,3:T(8,128)} %copy.28), calls=%async_computation.1 | async-start | bytes 9437184 | tf_op jit(solution)/shard_map/all_to_all | solution.py:127
  276.5 54.1 %all-to-all-done.1 = f32[2,32,384,48]{2,1,0,3:T(8,128)} async-done(((f32[2,32,384,48]{2,1,0,3:T(8,128)}), f32[2,32,384,48]{2,1,0,3:T(8,128)}, u32[]{:S(2)}, u32[]{:S(2)}) %all-to-all-start.1) | async-done | bytes 4718624 | tf_op jit(solution)/shard_map/all_to_all | solution.py:127
  333.5 8.0 %convolution_bitcast_fusion.1 = f32[2,512,384,3]{1,2,3,0:T(8,128)S(1)} fusion(f32[2,512,384,3]{2,1,3,0:T(8,128)S(1)} %bitcast.181, f32[512,512]{1,0:T(8,128)S(1)} %copy-done), kind=kOutput, calls=%fused_computation.78 | convolution fusion | flops 7247757312 | bytes 10485760 | tf_op jit(solution)/shard_map/cixy,ia->caxy/dot_general | solution.py:128
  350.5 7.2 %all-reduce.24 = (f32[4]{0:T(128)S(1)}, f32[4]{0:T(128)S(1)}, f32[4]{0:T(128)S(1)}, f32[4]{0:T(128)S(1)}) all-reduce(f32[4]{0:T(128)S(1)} %dynamic-update-slice, f32[4]{0:T(128)S(1)} %dynamic-update-slice.5, f32[4]{0:T(128)S(1)} %dynamic-update-slice.10, ...), channel_id=1, replica_groups=mesh['tm_0'=4,'tm_1'=2,'tm_2'=2,'space_0'=2,'space_1'=4] {'tm_0'}, use_global_device_ids=true, to_apply=%add.3 | all-reduce | flops 16 | bytes 128
  380.1 6.3 %all-reduce.26 = (f32[2]{0:T(128)S(1)}, f32[2]{0:T(128)S(1)}, f32[2]{0:T(128)S(1)}, f32[2]{0:T(128)S(1)}) all-reduce(f32[2]{0:T(128)S(1)} %dynamic-update-slice.2, f32[2]{0:T(128)S(1)} %dynamic-update-slice.7, f32[2]{0:T(128)S(1)} %dynamic-update-slice.12, ...), channel_id=1, replica_groups=mesh['tm_0'=4,'tm_1'=2,'tm_2'=2,'space_0'=2,'space_1'=4] {'tm_2'}, use_global_device_ids=true, to_apply=%add.5 | all-reduce | flops 8 | bytes 64
  406.5 6.6 %all-reduce.23 = (f32[4]{0:T(128)S(1)}, f32[4]{0:T(128)S(1)}, f32[4]{0:T(128)S(1)}, f32[4]{0:T(128)S(1)}) all-reduce(f32[4]{0:T(128)S(1)} %dynamic-update-slice.4, f32[4]{0:T(128)S(1)} %dynamic-update-slice.9, f32[4]{0:T(128)S(1)} %dynamic-update-slice.14, ...), channel_id=1, replica_groups=mesh['tm_0'=4,'tm_1'=2,'tm_2'=2,'space_0'=2,'space_1'=4] {'space_1'}, use_global_device_ids=true, to_apply=%add.7 | all-reduce | flops 16 | bytes 128
  415.7 7.2 %fusion.38 = f32[8,2,1,32,384,3]{4,3,1,0,5,2:T(8,128)S(1)} fusion(f32[8,2,32,512,1]{3,2,1,0,4:T(8,128)S(1)} %bitcast.173, f32[2,512,384,3]{1,2,3,0:T(8,128)} %copy-done.5, f32[]{:T(128)S(6)} %div.19, f32[3]{0:T(128)S(1)} %dynamic_slice.11, f32[512,384]{0,1:T(8,128)S(1)} %broadcast_add_fusion), kind=kOutput, calls=%fused_computation.81 | convolution fusion | flops 3626827776 | bytes 8912912 | tf_op jit(solution)/shard_map/caxy,ia->cixy/dot_general | solution.py:132
  423.1 8.8 %all_to_all.62 = f32[8,2,1,32,384,3]{4,3,0,5,2,1:T(8,128)S(1)} all-to-all(f32[8,2,1,32,384,3]{4,3,0,5,2,1:T(8,128)S(1)} %copy.33), channel_id=1, replica_groups=mesh['tm_0'=4,'tm_1'=2,'tm_2'=2,'space_0'=2,'space_1'=4] {'tm_2'}, dimensions={1} | all-to-all | bytes 4718592 | tf_op jit(solution)/shard_map/all_to_all | solution.py:45
  432.0 33.8 %all_to_all.63 = f32[8,2,1,32,384,3]{4,3,1,5,2,0:T(8,128)S(1)} all-to-all(f32[8,2,1,32,384,3]{4,3,1,5,2,0:T(8,128)S(1)} %copy.34), channel_id=1, replica_groups=mesh['tm_0'=4,'tm_1'=2,'tm_2'=2,'space_0'=2,'space_1'=4] {'tm_0','tm_1'}, dimensions={0} | all-to-all | bytes 4718592 | tf_op jit(solution)/shard_map/all_to_all | solution.py:45
  466.1 7.2 %fusion.41 = f32[1,32,384,48]{2,3,1,0:T(8,128)} fusion(f32[32,384,48]{1,0,2:T(8,128)S(1)} %bitcast.183, f32[384,384]{1,0:T(8,128)S(1)} %copy-done.7), kind=kOutput, calls=%fused_computation.82 | convolution fusion | flops 2717908992 | bytes 5308416 | tf_op jit(solution)/shard_map/ctby,jb->ctjy/dot_general | solution.py:134
  473.3 7.2 %copy.37 = f32[1,32,384,48]{3,1,0,2:T(8,128)} copy(f32[1,32,384,48]{2,3,1,0:T(8,128)} %fusion.41) | data formatting | bytes 4718592 | tf_op jit(solution)/shard_map/ctby,jb->ctjy/transpose | solution.py:134
  480.5 9.5 %reshape.403 = f32[8,1,73728]{2,1,0:T(1,128)} reshape(f32[384,1,32,48]{3,2,1,0:T(8,128)} %bitcast.179) | data formatting | bytes 4718592
  504.3 19.1 %all-to-all-done.4 = f32[8,1,73728]{2,1,0:T(1,128)} async-done(((f32[8,1,73728]{2,1,0:T(1,128)}), f32[8,1,73728]{2,1,0:T(1,128)}, u32[]{:S(2)}, u32[]{:S(2)}) %all-to-all-start.4) | async-done | bytes 2359328 | tf_op jit(solution)/shard_map/all_to_all | solution.py:135
  523.5 9.3 %reduce.49 = f32[8,73728]{1,0:T(8,128)} reduce(f32[8,1,73728]{2,1,0:T(1,128)} %all-to-all-done.4, f32[]{:T(128)} %broadcast.79), dimensions={1}, to_apply=%all_to_all.53.reduce_sub_computation | reduce | bytes 4718596 | tf_op jit(solution)/shard_map/all_to_all | solution.py:135
  532.8 6.9 %reshape.404 = f32[384,1,32,48]{3,2,1,0:T(8,128)} reshape(f32[8,73728]{1,0:T(8,128)} %reduce.49) | data formatting | bytes 4718592
  539.6 9.3 %copy.53 = f32[1,32,8,48,48]{4,2,3,1,0:T(8,128)} copy(f32[1,32,8,48,48]{4,1,3,2,0:T(8,128)} %bitcast.177) | data formatting | bytes 4718592 | tf_op jit(solution)/shard_map/all_to_all | solution.py:135
  548.9 5.9 %reshape.281 = f32[32,48,384]{2,1,0:T(8,128)} reshape(f32[1,32,48,8,48]{4,3,2,1,0:T(8,128)} %bitcast.178) | data formatting | bytes 4718592 | tf_op jit(solution)/shard_map/reshape.193
  554.8 7.2 %multiply_add_fusion.3 = f32[32,48,384]{2,1,0:T(8,128)} fusion(f32[32,48,384]{2,1,0:T(8,128)S(1)} %copy-done.3, f32[32,48,384]{2,1,0:T(8,128)} %reshape.281, f32[]{:T(128)S(6)} %div.23, f32[384,384]{1,0:T(8,128)} %param.17), kind=kOutput, calls=%fused_computation.72 | convolution fusion | flops 2719088640 | bytes 7667716 | tf_op jit(solution)/shard_map/ctxa,ka->ctxk/dot_general | solution.py:136
  (130 shorter events, 97.7 us)
Async XLA Ops:
  0.6 332.8 %copy-start = (f32[512,512]{1,0:T(8,128)S(1)}, f32[512,512]{1,0:T(8,128)}, u32[]{:S(2)}) copy-start(f32[512,512]{1,0:T(8,128)} %param.16) | copy-start | bytes 3145732
  1.8 11.0 %collective-permute-start = (f32[3,48,384]{2,1,0:T(8,128)S(1)}, f32[3,48,384]{2,1,0:T(8,128)S(1)}, u32[]{:S(2)}, u32[]{:S(2)}) collective-permute-start(f32[3,48,384]{2,1,0:T(8,128)S(1)} %get-tuple-element.47), channel_id=1, source_target_pairs={{0,8},{8,16},{16,24},{24,32},{32,40},{40,48},{48,56},{56,64},{64,7... | collective-permute-start | bytes 663560 | tf_op jit(solution)/shard_map/ppermute | solution.py:21
  7.8 8.8 %collective-permute-start.1 = (f32[3,48,384]{2,1,0:T(8,128)S(1)}, f32[3,48,384]{2,1,0:T(8,128)S(1)}, u32[]{:S(2)}, u32[]{:S(2)}) collective-permute-start(f32[3,48,384]{2,1,0:T(8,128)S(1)} %get-tuple-element.46), channel_id=1, source_target_pairs={{8,0},{16,8},{24,16},{32,24},{40,32},{48,40},{56,48},{64,56},{72,6... | collective-permute-start | bytes 663560 | tf_op jit(solution)/shard_map/ppermute | solution.py:23
  12.8 8.4 %copy-start.9 = (f32[2,4,512]{2,1,0:T(4,128)S(1)}, f32[2,4,512]{2,1,0:T(4,128)}, u32[]{:S(2)}) copy-start(f32[2,4,512]{2,1,0:T(4,128)} %param.14) | copy-start | bytes 49156
  12.8 8.5 %copy-start.8 = (f32[2,4,384]{2,1,0:T(4,128)S(1)}, f32[2,4,384]{2,1,0:T(4,128)}, u32[]{:S(2)}) copy-start(f32[2,4,384]{2,1,0:T(4,128)} %param.15) | copy-start | bytes 36868
  16.7 6.2 %collective-permute-start.2 = (f32[38,3,384]{2,1,0:T(4,128)S(1)}, f32[38,3,384]{2,1,0:T(4,128)S(1)}, u32[]{:S(2)}, u32[]{:S(2)}) collective-permute-start(f32[38,3,384]{2,1,0:T(4,128)S(1)} %get-tuple-element.44), channel_id=1, source_target_pairs={{0,1},{1,2},{2,3},{3,4},{4,5},{5,6},{6,7},{8,9},{9,10},{10,11},{11... | collective-permute-start | bytes 525320 | tf_op jit(solution)/shard_map/ppermute | solution.py:21
  19.9 6.8 %collective-permute-start.3 = (f32[38,3,384]{2,1,0:T(4,128)S(1)}, f32[38,3,384]{2,1,0:T(4,128)S(1)}, u32[]{:S(2)}, u32[]{:S(2)}) collective-permute-start(f32[38,3,384]{2,1,0:T(4,128)S(1)} %get-tuple-element.45), channel_id=1, source_target_pairs={{1,0},{2,1},{3,2},{4,3},{5,4},{6,5},{7,6},{9,8},{10,9},{11,10},{12... | collective-permute-start | bytes 525320 | tf_op jit(solution)/shard_map/ppermute | solution.py:23
  59.0 12.2 %copy-start.1 = (f32[38,54,384]{2,1,0:T(8,128)S(1)}, f32[38,54,384]{2,1,0:T(8,128)}, u32[]{:S(2)}) copy-start(f32[38,54,384]{2,1,0:T(8,128)} %get-tuple-element.42) | copy-start | bytes 9455620
  59.0 12.2 %copy-start.2 = (f32[38,54,384]{2,1,0:T(8,128)S(1)}, f32[38,54,384]{2,1,0:T(8,128)}, u32[]{:S(2)}) copy-start(f32[38,54,384]{2,1,0:T(8,128)} %get-tuple-element.43) | copy-start | bytes 9455620
  77.1 18.0 %copy-start.6 = (f32[32,48,384]{2,1,0:T(8,128)S(1)}, f32[32,48,384]{2,1,0:T(8,128)}, u32[]{:S(2)}) copy-start(f32[32,48,384]{2,1,0:T(8,128)} %param.11) | copy-start | bytes 7077892
  77.1 18.0 %copy-start.7 = (f32[384,384]{1,0:T(8,128)S(1)}, f32[384,384]{1,0:T(8,128)}, u32[]{:S(2)}) copy-start(f32[384,384]{1,0:T(8,128)} %param.17) | copy-start | bytes 1769476
  93.7 1.4 copy-start.4
  261.2 13.0 %copy-start.10 = (f32[384]{0:T(512)S(1)}, f32[384]{0:T(512)}, u32[]{:S(2)}) copy-start(f32[384]{0:T(512)} %param.19) | copy-start | bytes 4612
  261.2 13.0 %copy-start.16 = (u32[128]{0:T(128)S(1)}, u32[128]{0:T(128)}, u32[]{:S(2)}) copy-start(u32[128]{0:T(128)} %constant.53) | copy-start | bytes 1540
  261.2 13.7 %copy-start.11 = (f32[512]{0:T(512)S(1)}, f32[512]{0:T(512)}, u32[]{:S(2)}) copy-start(f32[512]{0:T(512)} %param.18) | copy-start | bytes 6148
  261.2 69.5 %all-to-all-start.1 = ((f32[2,32,384,48]{2,1,0,3:T(8,128)}), f32[2,32,384,48]{2,1,0,3:T(8,128)}, u32[]{:S(2)}, u32[]{:S(2)}) async-start(f32[2,32,384,48]{2,1,0,3:T(8,128)} %copy.28), calls=%async_computation.1 | async-start | bytes 9437184 | tf_op jit(solution)/shard_map/all_to_all | solution.py:127
  341.5 2.1 copy-start.5
  343.6 6.3 %copy-start.15 = (u32[128]{0:T(128)S(1)}, u32[128]{0:T(128)}, u32[]{:S(2)}) copy-start(u32[128]{0:T(128)} %constant.58) | copy-start | bytes 1540
  343.6 21.9 %copy-start.14 = (u32[128]{0:T(128)S(1)}, u32[128]{0:T(128)}, u32[]{:S(2)}) copy-start(u32[128]{0:T(128)} %constant.63) | copy-start | bytes 1540
  343.6 35.9 %copy-start.13 = (u32[128]{0:T(128)S(1)}, u32[128]{0:T(128)}, u32[]{:S(2)}) copy-start(u32[128]{0:T(128)} %constant.68) | copy-start | bytes 1540
  343.6 50.6 %copy-start.12 = (u32[128]{0:T(128)S(1)}, u32[128]{0:T(128)}, u32[]{:S(2)}) copy-start(u32[128]{0:T(128)} %constant.73) | copy-start | bytes 1540
  490.0 8.5 %copy-start.3 = (f32[32,48,384]{2,1,0:T(8,128)S(1)}, f32[32,48,384]{2,1,0:T(8,128)}, u32[]{:S(2)}) copy-start(f32[32,48,384]{2,1,0:T(8,128)} %param.12) | copy-start | bytes 7077892
  490.0 33.5 %all-to-all-start.4 = ((f32[8,1,73728]{2,1,0:T(1,128)}), f32[8,1,73728]{2,1,0:T(1,128)}, u32[]{:S(2)}, u32[]{:S(2)}) async-start(f32[8,1,73728]{2,1,0:T(1,128)} %reshape.403), calls=%async_computation.4 | async-start | bytes 4718592 | tf_op jit(solution)/shard_map/all_to_all | solution.py:135
